TPU v7x, 32 devices: a whole 2x2x4 slice. The times are simulated.
32 devices in a mesh: blk: 4 (over x, core), grp: 8 (over z, y).
Axes of the slice: x: 2, y: 2, z: 4, core: 2. Of those that a mesh axis runs over, the one named last changes fastest.
Arguments:
- design: float32 [8, 4096], P(None, ('blk', 'grp')), may hold values from -5 to 5
- lengthscales: float32 [8], replicated, may hold values from 0.55 to 0.85
- counts: int32 [4096], P(('blk', 'grp')), may hold values from 1 to 16
- noise_base: float32 [1], replicated, may hold values from 0.5 to 2
- targets: float32 [16, 4096], P(None, ('blk', 'grp')), may hold values from -6 to 6
Outputs:
- solution: float32 [16, 4096], P(None, ('blk', 'grp'))
- residual: float32 [16, 4096], P(None, ('blk', 'grp'))
- image: float32 [16, 4096], P(None, ('blk', 'grp'))
All inputs are finite; a program needn't handle non-finite values.
Results may differ from a plain program's by a relative error of at most 0.0003.
Values sent between devices are 32-bit elements; how exact they have to be, the bound alone decides.
No kernel may reach another device: no remote copies, remote signals or barrier semaphores. Data moves between devices by JAX's collectives and lax.ppermute only.
A program may use at most 64 MiB of HBM per device.

v0:
```python
import math

import jax
import jax.numpy as jnp
from jax import lax
from jax.sharding import PartitionSpec as P

ROOT_FIVE = 2.23606797749979


def kernel_terms(own_scaled, own_square, col_scaled, col_dirs, running):
    columns = col_scaled.shape[1]
    block_width = math.gcd(columns, 2048)
    block_count = columns // block_width

    def advance(block_index, partial_sum):
        offset = block_index * block_width
        chosen = lax.dynamic_slice_in_dim(col_scaled, offset, block_width, 1)
        chosen_dirs = lax.dynamic_slice_in_dim(col_dirs, offset, block_width, 1)
        chosen_square = jnp.sum(chosen * chosen, 0)
        inner_products = jnp.einsum(
            "dr,dc->rc", own_scaled, chosen, precision=lax.Precision.HIGHEST
        )
        dist_square = jnp.maximum(
            own_square[:, None] + chosen_square[None, :] - 2.0 * inner_products, 0.0
        )
        radius = jnp.sqrt(dist_square)
        kernel_tile = (1.0 + ROOT_FIVE * radius + 5.0 / 3.0 * dist_square) * jnp.exp(
            -ROOT_FIVE * radius
        )
        return partial_sum + jnp.einsum(
            "kc,rc->kr", chosen_dirs, kernel_tile, precision=lax.Precision.HIGHEST
        )

    return lax.fori_loop(0, block_count, advance, running)


def on_device(design, lengthscales, counts, noise_base, targets):
    scaled = design / lengthscales[:, None]
    own_square = jnp.sum(scaled * scaled, 0)
    noise_diag = noise_base[0] / counts.astype(jnp.float32)

    def operator_apply(direction):
        zero_start = jnp.zeros(direction.shape, jnp.float32)
        group_points, group_dirs = (
            lax.all_gather(scaled, "grp", axis=1, tiled=True),
            lax.all_gather(direction, "grp", axis=1, tiled=True),
        )
        product_sum = kernel_terms(
            scaled,
            own_square,
            lax.all_gather(group_points, "blk", axis=1, tiled=True),
            lax.all_gather(group_dirs, "blk", axis=1, tiled=True),
            zero_start,
        )
        return product_sum + noise_diag[None, :] * direction

    first = operator_apply(targets)
    local_gammas = jnp.sum(targets * targets, 1)
    local_deltas = jnp.sum(first * targets, 1)
    gammas, deltas = lax.psum((local_gammas, local_deltas), ("blk", "grp"))
    further = operator_apply(first)
    alphas = (gammas / deltas)[:, None]
    solution = alphas * targets
    residual = targets - alphas * first
    image = first - alphas * further
    return (solution, residual, image)


def solution(mesh):
    in_specs = (P(None, ("blk", "grp")), P(), P(("blk", "grp")), P(), P(None, ("blk", "grp")))
    out_specs = (P(None, ("blk", "grp")), P(None, ("blk", "grp")), P(None, ("blk", "grp")))
    return jax.shard_map(
        on_device, mesh=mesh, in_specs=in_specs, out_specs=out_specs, check_vma=False
    )
```

profile of v0, /device:TPU:0, one launch (start us, length us, event | category | flops | bytes accessed | tf_op | source)
XLA Modules:
  0.0 167.1 jit_solution(15107459266311778984)
XLA Ops:
  0.6 0.0 copy-start.1
  1.3 0.0 copy-start.3
  1.3 0.6 copy-done.3
  2.0 0.0 copy-start.2
  2.0 0.0 copy-done.1
  2.0 0.6 copy-done.2
  2.6 0.1 multiply_reduce_fusion.4
  2.7 0.0 copy-start
  2.7 32.6 %all_gather.22 = f32[8,1024]{1,0:T(8,128)S(1)} all-gather(f32[8,128]{1,0:T(8,128)S(1)} %get-tuple-element.408), channel_id=1, replica_groups=mesh['blk'=4,'grp'=8] {'grp'}, dimensions={1}, use_global_device_ids=true | all-gather | bytes 36864 | tf_op jit(solution)/shard_map/all_gather | solution.py:46
  35.3 0.0 copy-done
  35.3 30.5 %all_gather.20 = f32[16,1024]{1,0:T(8,128)S(1)} all-gather(f32[16,128]{1,0:T(8,128)S(1)} %copy-done), channel_id=1, replica_groups=mesh['blk'=4,'grp'=8] {'grp'}, dimensions={1}, use_global_device_ids=true | all-gather | bytes 73728 | tf_op jit(solution)/shard_map/all_gather | solution.py:47
  65.8 5.4 %all_gather.23 = f32[8,4096]{1,0:T(8,128)S(1)} all-gather(f32[8,1024]{1,0:T(8,128)S(1)} %all_gather.22), channel_id=1, replica_groups=mesh['blk'=4,'grp'=8] {'blk'}, dimensions={1}, use_global_device_ids=true | all-gather | bytes 163840 | tf_op jit(solution)/shard_map/all_gather | solution.py:52
  71.2 5.8 %all_gather.21 = f32[16,4096]{1,0:T(8,128)S(1)} all-gather(f32[16,1024]{1,0:T(8,128)S(1)} %all_gather.20), channel_id=1, replica_groups=mesh['blk'=4,'grp'=8] {'blk'}, dimensions={1}, use_global_device_ids=true | all-gather | bytes 327680 | tf_op jit(solution)/shard_map/all_gather | solution.py:53
  77.0 6.3 %while.28 = (s32[]{:T(128)}, f32[16,128]{1,0:T(8,128)S(1)}, f32[16,4096]{1,0:T(8,128)S(1)}, f32[128]{0:T(128)S(1)}, f32[8,4096]{1,0:T(8,128)S(1)}, /*index=5*/f3...) while((s32[]{:T(128)}, f32[16,128]{1,0:T(8,128)S(1)}, ...), condition=%wide.region_5.0_spmd.clone, body=%wide.region_3.5_spmd.clone.sunk | while | flops 78153728 | bytes 2396849 | solution.py:35
  77.1 2.0 %fusion.62 = f32[128,2048]{0,1:T(8,128)S(1)} fusion(f32[8,128]{1,0:T(8,128)S(1)} %get-tuple-element.398, f32[2048]{0:T(1024)S(1)} %multiply_reduce_fusion.7, f32[128]{0:T(128)S(1)} %get-tuple-element.396, f32[8,4096]{1,0:T(8,128)S(1)} %get-tuple-element.397, s32[]{:T(128)S(6)} %select_n.20), kind=kOutput, calls=%fused_computation.3.clone.1 | convolution fusion | flops 26214400 | bytes 1126916 | tf_op jit(solution)/shard_map/while/body/eval_jaxpr/dr,dc->rc/dot_general | solution.py:21
  79.1 1.1 convolution_add_fusion.4
  80.2 2.0 %fusion.62 = f32[128,2048]{0,1:T(8,128)S(1)} fusion(f32[8,128]{1,0:T(8,128)S(1)} %get-tuple-element.398, f32[2048]{0:T(1024)S(1)} %multiply_reduce_fusion.7, f32[128]{0:T(128)S(1)} %get-tuple-element.396, f32[8,4096]{1,0:T(8,128)S(1)} %get-tuple-element.397, s32[]{:T(128)S(6)} %select_n.20), kind=kOutput, calls=%fused_computation.3.clone.1 | convolution fusion | flops 26214400 | bytes 1126916 | tf_op jit(solution)/shard_map/while/body/eval_jaxpr/dr,dc->rc/dot_general | solution.py:21
  82.2 1.1 convolution_add_fusion.4
  83.4 0.1 multiply_reduce_fusion.2
  83.5 39.5 %all-reduce = (f32[16]{0:T(128)S(1)}, f32[16]{0:T(128)S(1)}) all-reduce(f32[16]{0:T(128)S(1)} %get-tuple-element.266, f32[16]{0:T(128)S(1)} %get-tuple-element.265), channel_id=1, replica_groups=mesh['blk'=4,'grp'=8] {'blk','grp'}, use_global_device_ids=true, to_apply=%region_1.2 | all-reduce | flops 32 | bytes 256 | tf_op jit(solution)/shard_map/psum | solution.py:61
  123.0 30.5 %all_gather.24 = f32[16,1024]{1,0:T(8,128)S(1)} all-gather(f32[16,128]{1,0:T(8,128)S(1)} %get-tuple-element.293), channel_id=1, replica_groups=mesh['blk'=4,'grp'=8] {'grp'}, dimensions={1}, use_global_device_ids=true | all-gather | bytes 73728 | tf_op jit(solution)/shard_map/all_gather | solution.py:47
  153.6 6.5 %all_gather.25 = f32[16,4096]{1,0:T(8,128)S(1)} all-gather(f32[16,1024]{1,0:T(8,128)S(1)} %all_gather.24), channel_id=1, replica_groups=mesh['blk'=4,'grp'=8] {'blk'}, dimensions={1}, use_global_device_ids=true | all-gather | bytes 327680 | tf_op jit(solution)/shard_map/all_gather | solution.py:53
  160.1 6.3 %while.29 = (s32[]{:T(128)}, f32[16,128]{1,0:T(8,128)S(1)}, f32[16,4096]{1,0:T(8,128)S(1)}, f32[128]{0:T(128)S(1)}, f32[8,4096]{1,0:T(8,128)S(1)}, /*index=5*/f3...) while((s32[]{:T(128)}, f32[16,128]{1,0:T(8,128)S(1)}, ...), condition=%wide.region_10.0_spmd.clone, body=%wide.region_8.0_spmd.clone.sunk | while | flops 78153728 | bytes 2396849 | solution.py:35
  160.1 2.0 %fusion.67 = f32[128,2048]{0,1:T(8,128)S(1)} fusion(f32[8,128]{1,0:T(8,128)S(1)} %get-tuple-element.428, f32[2048]{0:T(1024)S(1)} %multiply_reduce_fusion.8, f32[128]{0:T(128)S(1)} %get-tuple-element.426, f32[8,4096]{1,0:T(8,128)S(1)} %get-tuple-element.427, s32[]{:T(128)S(6)} %select_n.21), kind=kOutput, calls=%fused_computation.29.clone.1 | convolution fusion | flops 26214400 | bytes 1126916 | tf_op jit(solution)/shard_map/while/body/eval_jaxpr/dr,dc->rc/dot_general | solution.py:21
  162.1 1.1 convolution_add_fusion.5
  163.3 2.0 %fusion.67 = f32[128,2048]{0,1:T(8,128)S(1)} fusion(f32[8,128]{1,0:T(8,128)S(1)} %get-tuple-element.428, f32[2048]{0:T(1024)S(1)} %multiply_reduce_fusion.8, f32[128]{0:T(128)S(1)} %get-tuple-element.426, f32[8,4096]{1,0:T(8,128)S(1)} %get-tuple-element.427, s32[]{:T(128)S(6)} %select_n.21), kind=kOutput, calls=%fused_computation.29.clone.1 | convolution fusion | flops 26214400 | bytes 1126916 | tf_op jit(solution)/shard_map/while/body/eval_jaxpr/dr,dc->rc/dot_general | solution.py:21
  165.3 1.1 convolution_add_fusion.5
  166.4 0.7 multiply_subtract_fusion
  (8 shorter events, 0.1 us)
Async XLA Ops:
  0.6 1.3 copy-start.1
  1.3 0.7 copy-start.3
  2.0 0.7 copy-start.2
  2.7 32.6 %copy-start = (f32[16,128]{1,0:T(8,128)S(1)}, f32[16,128]{1,0:T(8,128)}, u32[]{:S(2)}) copy-start(f32[16,128]{1,0:T(8,128)} %param.13) | copy-start | bytes 24580
where the time goes:
time: 168 us; the launch traced here: 167 us
  blocking collectives  151 us (90%)
  matrix products  12.4 us (7%)
    all_gather x2, blocking collectives, operator_apply(): lax.all_gather(direction, 'grp', axis=1, tiled=True)  61.1 us
    psum x1, blocking collectives, on_device(): gammas, deltas = lax.psum((local_gammas, local_deltas), ('blk', 'grp'))  39.5 us
    all_gather x1, blocking collectives, operator_apply(): lax.all_gather(scaled, 'grp', axis=1, tiled=True)  32.6 us
    all_gather x2, blocking collectives, operator_apply(): lax.all_gather(group_dirs, 'blk', axis=1, tiled=True)  12.4 us
    dot_general x4, matrix products, advance(): jnp.einsum('dr,dc->rc', own_scaled, chosen, precision=lax.Precision.HIGHEST)  7.95 us
    all_gather x1, blocking collectives, operator_apply(): lax.all_gather(group_points, 'blk', axis=1, tiled=True)  5.4 us
    dot_general x4, matrix products, advance(): jnp.einsum('kc,rc->kr', chosen_dirs, kernel_tile, precision=lax.Precision...  4.49 us

commit v1 on v0

v1 whole, which is shorter than its diff:
```python
import functools

import jax
import jax.numpy as jnp
from jax import lax
from jax.experimental import pallas as pl
from jax.experimental.pallas import tpu as pltpu
from jax.sharding import PartitionSpec as P

ROOT_FIVE = 2.23606797749979
AXES = ("blk", "grp")
TINY = 1e-30


def split3(x):
    high = x.astype(jnp.bfloat16)
    rest = x - high.astype(jnp.float32)
    middle = rest.astype(jnp.bfloat16)
    low = (rest - middle.astype(jnp.float32)).astype(jnp.bfloat16)
    return high, middle, low


def split2(x):
    high = x.astype(jnp.bfloat16)
    return high, (x - high.astype(jnp.float32)).astype(jnp.bfloat16)


def augment(points, own):
    high, middle, low = split3(points)
    squares = jnp.sum(points * points, 0, keepdims=True)
    sq = split3(jnp.broadcast_to(squares, points.shape))
    one = jnp.ones(points.shape, jnp.bfloat16)
    row = lax.broadcasted_iota(jnp.int32, points.shape, 0)

    def pick(parts):
        a, b, c = (part.astype(jnp.float32) for part in parts)
        zero = jnp.zeros(points.shape, jnp.float32)
        return jnp.where(row == 0, a, jnp.where(row == 1, b, jnp.where(row == 2, c, zero))).astype(jnp.bfloat16)

    if own:
        high, middle, low = (part * jnp.bfloat16(-2.0) for part in (high, middle, low))
        parts = [high, high, middle, high, low, middle, pick(sq), one]
    else:
        parts = [high, middle, high, low, high, middle, one, pick(sq)]
    return jnp.concatenate(parts, 0)


def matern(dist):
    dist = jnp.maximum(dist, TINY)
    radius = ROOT_FIVE * (dist * lax.rsqrt(dist))
    return (1.0 + radius + (5.0 / 3.0) * dist) * jnp.exp(-radius)


def dot_nt(a, b):
    return lax.dot_general(a, b, (((1,), (1,)), ((), ())), preferred_element_type=jnp.float32)


def dot_tn(a, b):
    return lax.dot_general(a, b, (((0,), (0,)), ((), ())), preferred_element_type=jnp.float32)


def first_kernel(dim, width, own_ref, scale_ref, noise_ref, all_ref, first_ref, high_ref, low_ref):
    blocks = all_ref.shape[0]
    columns = all_ref.shape[2]
    rhs = all_ref.shape[1] - dim
    scale = scale_ref[...]
    own = augment(own_ref[0:dim, :] / scale, True)
    total = jnp.zeros((own_ref.shape[1], 2 * rhs), jnp.float32)
    for start in range(0, blocks, width):
        points = jnp.concatenate([all_ref[start + k, 0:dim, :] for k in range(width)], 1)
        vectors = jnp.concatenate([all_ref[start + k, dim:, :] for k in range(width)], 1)
        tile = matern(dot_tn(own, augment(points / scale, False)))
        high, low = split2(tile)
        place = pl.ds(start * columns, width * columns)
        high_ref[:, place] = high
        low_ref[:, place] = low
        v_high, v_low = split2(vectors)
        total = total + dot_nt(high, jnp.concatenate([v_high, v_low], 0))
        total = total + dot_nt(low, jnp.concatenate([v_high, jnp.zeros_like(v_low)], 0))
    product = total[:, 0:rhs] + total[:, rhs:]
    first_ref[...] = product.T + noise_ref[...] * own_ref[dim:, :]


def last_kernel(dim, width, own_ref, first_ref, noise_ref, all_ref, firsts_ref, high_ref, low_ref,
                solution_ref, residual_ref, image_ref):
    blocks = all_ref.shape[0]
    columns = all_ref.shape[2]
    rhs = all_ref.shape[1] - dim
    total = jnp.zeros((high_ref.shape[0], 2 * rhs), jnp.float32)
    gammas = jnp.zeros((rhs, columns), jnp.float32)
    deltas = jnp.zeros((rhs, columns), jnp.float32)
    for start in range(0, blocks, width):
        for k in range(width):
            target = all_ref[start + k, dim:, :]
            gammas = gammas + target * target
            deltas = deltas + target * firsts_ref[start + k]
        vectors = jnp.concatenate([firsts_ref[start + k] for k in range(width)], 1)
        place = pl.ds(start * columns, width * columns)
        v_high, v_low = split2(vectors)
        total = total + dot_nt(high_ref[:, place], jnp.concatenate([v_high, v_low], 0))
        total = total + dot_nt(low_ref[:, place], jnp.concatenate([v_high, jnp.zeros_like(v_low)], 0))
    product = total[:, 0:rhs] + total[:, rhs:]
    first = first_ref[...]
    targets = own_ref[dim:, :]
    further = product.T + noise_ref[...] * first
    alphas = jnp.sum(gammas, 1, keepdims=True) / jnp.sum(deltas, 1, keepdims=True)
    solution_ref[...] = alphas * targets
    residual_ref[...] = targets - alphas * first
    image_ref[...] = first - alphas * further


def gather(x, size):
    return lax.all_to_all(jnp.broadcast_to(x[None], (size,) + x.shape), AXES, 0, 0)


def on_device(size, design, lengthscales, counts, noise_base, targets):
    dim, own = design.shape
    rhs = targets.shape[0]
    points = size * own
    noise = (noise_base[0] / counts.astype(jnp.float32))[None, :]
    packed = jnp.concatenate([design, targets], 0)
    everything = gather(packed, size)
    width = 4
    first, high, low = pl.pallas_call(
        functools.partial(first_kernel, dim, width),
        out_shape=(
            jax.ShapeDtypeStruct((rhs, own), jnp.float32),
            jax.ShapeDtypeStruct((own, points), jnp.bfloat16),
            jax.ShapeDtypeStruct((own, points), jnp.bfloat16),
        ),
        name="first_apply",
    )(packed, lengthscales[:, None], noise, everything)
    firsts = gather(first, size)
    shape = jax.ShapeDtypeStruct((rhs, own), jnp.float32)
    return pl.pallas_call(
        functools.partial(last_kernel, dim, width),
        out_shape=(shape, shape, shape),
        name="second_apply",
    )(packed, first, noise, everything, firsts, high, low)


def solution(mesh):
    size = mesh.shape["blk"] * mesh.shape["grp"]
    in_specs = (P(None, AXES), P(), P(AXES), P(), P(None, AXES))
    out_specs = (P(None, AXES), P(None, AXES), P(None, AXES))
    return jax.shard_map(
        functools.partial(on_device, size), mesh=mesh, in_specs=in_specs, out_specs=out_specs, check_vma=False
    )
```

time: 168 us -> 44.9 us (0.27)
  blocking collectives: 151 us -> 12.8 us
  matrix products: 12.4 us -> 0 us
  waiting for transfers between devices: 0 us -> 10.2 us
  starting transfers between devices: 0 us -> 7.33 us
  Pallas kernels: 0 us -> 7.31 us
  local copies, waits for them, and re-layouts: 1.3 us -> 4.91 us
    all_gather x6 -> x0, blocking collectives: 111 us -> none  [the longest x2 61.1 us: operator_apply(): lax.all_gather(direction, 'grp', axis=1, tiled=True)]
    psum x1 -> x0, blocking collectives: 39.5 us -> none  [on_device(): gammas, deltas = lax.psum((local_gammas, local_deltas), ('blk', 'grp'))]
    all_to_all x0 -> x1, blocking collectives: none -> 12.8 us  [gather(): lax.all_to_all(jnp.broadcast_to(x[None], (size,) + x.shape), AXES, 0, 0)]
    dot_general x8 -> x0, matrix products: 12.4 us -> none  [the longest x4 7.95 us: advance(): jnp.einsum('dr,dc->rc', own_scaled, chosen, precision=lax.Precision.HIGHEST)]
    all_to_all x0 -> x1, waiting for transfers between devices: none -> 10.2 us  [gather(): lax.all_to_all(jnp.broadcast_to(x[None], (size,) + x.shape), AXES, 0, 0)]
    all_to_all x0 -> x1, starting transfers between devices: none -> 7.33 us  [gather(): lax.all_to_all(jnp.broadcast_to(x[None], (size,) + x.shape), AXES, 0, 0)]
    pallas_call x0 -> x2, Pallas kernels: none -> 7.31 us  [the longest x1 4.12 us: on_device(): pl.pallas_call(functools.partial(first_kernel, dim, width), out_shape=(ja...]
    broadcast_in_dim x0 -> x3, local copies, waits for them, and re-layouts: none -> 2.16 us  [the longest x2 1.48 us: gather(): jnp.broadcast_to(x[None], (size,) + x.shape)]
  transfers between devices with their start and end apart: 0 -> 1, of which waited for: 0 -> 1; matrix products, arithmetic and copies ran while one was open for 0% -> 3% of each run, Pallas kernels for 0% -> 0%
where the time goes in v1:
time: 44.9 us; the launch traced here: 44.5 us
  blocking collectives  12.8 us (29%)
  waiting for transfers between devices  10.2 us (23%)
  starting transfers between devices  7.33 us (16%)
  Pallas kernels  7.31 us (16%)
  local copies, waits for them, and re-layouts  4.91 us (11%)
  between operations  1.31 us (3%)
  other arithmetic  0.58 us (1%)
    all_to_all x1, blocking collectives, gather(): lax.all_to_all(jnp.broadcast_to(x[None], (size,) + x.shape), AXES, 0, 0)  12.8 us
    all_to_all x1, waiting for transfers between devices, gather(): lax.all_to_all(jnp.broadcast_to(x[None], (size,) + x.shape), AXES, 0, 0)  10.2 us
    all_to_all x1, starting transfers between devices, gather(): lax.all_to_all(jnp.broadcast_to(x[None], (size,) + x.shape), AXES, 0, 0)  7.33 us
    pallas_call x1, Pallas kernels, on_device(): pl.pallas_call(functools.partial(first_kernel, dim, width), out_shape=(ja...  4.12 us
    pallas_call x1, Pallas kernels, on_device(): pl.pallas_call(functools.partial(last_kernel, dim, width), out_shape=(sha...  3.19 us
    unnamed x11, local copies, waits for them, and re-layouts  2.75 us
    broadcast_in_dim x2, local copies, waits for them, and re-layouts, gather(): jnp.broadcast_to(x[None], (size,) + x.shape)  1.48 us
  transfers between devices with their start and end apart: 1, of which 1 were waited for; matrix products, arithmetic and copies ran while one was open for 3% of the time, Pallas kernels for 0%

profile of v1, /device:TPU:0, one launch (start us, length us, event | category | flops | bytes accessed | tf_op | source)
XLA Modules:
  0.0 44.5 jit_solution(16195402779989874294)
XLA Ops:
  0.6 0.0 copy-start.2
  0.6 0.7 %constant_dynamic-update-slice_fusion.1 = f32[24,128]{1,0:T(8,128)S(1)} fusion(f32[8,128]{1,0:T(8,128)} %param.5), kind=kLoop, calls=%fused_computation.1 | loop fusion | bytes 8192
  1.3 0.0 copy-done.2
  1.3 0.0 copy-start.1
  1.3 0.8 %broadcast_in_dim.20 = f32[32,24,128]{2,1,0:T(8,128)} broadcast(f32[24,128]{1,0:T(8,128)S(1)} %constant_dynamic-update-slice_fusion.own_ref), dimensions={1,2} | broadcast | bytes 405504 | tf_op jit(solution)/shard_map/broadcast_in_dim | solution.py:113
  2.1 0.0 copy-done.1
  2.1 7.3 %all-to-all-start = ((f32[32,24,128]{2,1,0:T(8,128)}), f32[32,24,128]{2,1,0:T(8,128)S(1)}, u32[]{:S(2)}, u32[]{:S(2)}) async-start(f32[32,24,128]{2,1,0:T(8,128)} %broadcast_in_dim.20), calls=%async_computation | async-start | bytes 786432 | tf_op jit(solution)/shard_map/all_to_all | solution.py:113
  10.1 0.0 copy-start.3
  10.1 0.6 %copy-done.3 = f32[8]{0:T(128)S(1)} copy-done((f32[8]{0:T(128)S(1)}, f32[8]{0:T(128)}, u32[]{:S(2)}) %copy-start.3) | copy-done | bytes 56
  10.8 0.7 %copy.8.scale_ref = f32[8,1]{1,0:T(8,128)} copy(f32[8,1]{0,1:T(1,128)S(1)} %bitcast.5) | data formatting | bytes 64 | tf_op jit(solution)/shard_map/broadcast_in_dim | solution.py:132
  11.4 0.0 copy-start.4
  11.4 0.7 %copy-done.4 = s32[128]{0:T(128)S(1)} copy-done((s32[128]{0:T(128)S(1)}, s32[128]{0:T(128)}, u32[]{:S(2)}) %copy-start.4) | copy-done | bytes 536
  12.1 0.6 %divide_bitcast_fusion.noise_ref = f32[1,128]{1,0:T(1,128)} fusion(s32[128]{0:T(128)S(1)} %copy-done.4, f32[]{:T(128)} %bitcast.4), kind=kLoop, calls=%fused_computation.2 | loop fusion | flops 256 | bytes 1028 | tf_op jit(solution)/shard_map/broadcast_in_dim | solution.py:120
  12.7 10.2 %all-to-all-done.all_ref = f32[32,24,128]{2,1,0:T(8,128)S(1)} async-done(((f32[32,24,128]{2,1,0:T(8,128)}), f32[32,24,128]{2,1,0:T(8,128)S(1)}, u32[]{:S(2)}, u32[]{:S(2)}) %all-to-all-start) | async-done | bytes 393248 | tf_op jit(solution)/shard_map/all_to_all | solution.py:113
  22.9 0.0 copy-start
  22.9 0.7 %copy-done = f32[32,24,128]{2,1,0:T(8,128)} copy-done((f32[32,24,128]{2,1,0:T(8,128)}, f32[32,24,128]{2,1,0:T(8,128)S(1)}, u32[]{:S(2)}) %copy-start) | copy-done | bytes 393240
  23.6 4.1 %first_apply.1 = (f32[16,128]{1,0:T(8,128)}, bf16[128,4096]{1,0:T(8,128)(2,1)}, bf16[128,4096]{1,0:T(8,128)(2,1)}) custom-call(f32[24,128]{1,0:T(8,128)} %copy-done.1, f32[8,1]{1,0:T(8,128)} %copy.8.scale_ref, f32[1,128]{1,0:T(1,128)} %divide_bitcast_fusion.noise_ref, f32[32,24,128]{2,1,0:T(8,128)} %copy-done), custom_call_target="tpu_custom_call" | custom-call | tf_op jit(solution)/shard_map/first_apply/pallas_call | solution.py:124
  27.7 0.7 %broadcast_in_dim.21 = f32[32,16,128]{2,1,0:T(8,128)S(1)} broadcast(f32[16,128]{1,0:T(8,128)} %get-tuple-element.6.first_ref), dimensions={1,2} | broadcast | bytes 270336 | tf_op jit(solution)/shard_map/broadcast_in_dim | solution.py:113
  28.5 12.8 %all_to_all.10.firsts_ref = f32[32,16,128]{2,1,0:T(8,128)} all-to-all(f32[32,16,128]{2,1,0:T(8,128)S(1)} %broadcast_in_dim.21), channel_id=1, replica_groups=mesh['blk'=4,'grp'=8] {'blk','grp'}, dimensions={0} | all-to-all | bytes 524288 | tf_op jit(solution)/shard_map/all_to_all | solution.py:113
  41.3 3.2 %second_apply.1 = (f32[16,128]{1,0:T(8,128)}, f32[16,128]{1,0:T(8,128)}, f32[16,128]{1,0:T(8,128)}) custom-call(f32[24,128]{1,0:T(8,128)} %copy-done.1, f32[16,128]{1,0:T(8,128)} %get-tuple-element.6.first_ref, f32[1,128]{1,0:T(1,128)} %divide_bitcast_fusion.noise_ref, f32[32,24,128]{2,1,0:T(8,128)} %copy-done, f32[32,16,128]{2,1,0:T(8,128)} %all_to_all.10.firsts_ref, ...), custom_call_target="tpu_custom_call" | custom-call | tf_op jit(solution)/shard_map/second_apply/pallas_call | solution.py:135
  (1 shorter events, 0.0 us)
Async XLA Ops:
  0.6 0.7 %copy-start.2 = (f32[16,128]{1,0:T(8,128)S(1)}, f32[16,128]{1,0:T(8,128)}, u32[]{:S(2)}) copy-start(f32[16,128]{1,0:T(8,128)} %param.9) | copy-start | bytes 24580
  1.3 0.8 %copy-start.1 = (f32[24,128]{1,0:T(8,128)}, f32[24,128]{1,0:T(8,128)S(1)}, u32[]{:S(2)}) copy-start(f32[24,128]{1,0:T(8,128)S(1)} %constant_dynamic-update-slice_fusion.own_ref) | copy-start | bytes 36868
  2.1 20.8 %all-to-all-start = ((f32[32,24,128]{2,1,0:T(8,128)}), f32[32,24,128]{2,1,0:T(8,128)S(1)}, u32[]{:S(2)}, u32[]{:S(2)}) async-start(f32[32,24,128]{2,1,0:T(8,128)} %broadcast_in_dim.20), calls=%async_computation | async-start | bytes 786432 | tf_op jit(solution)/shard_map/all_to_all | solution.py:113
  10.1 0.7 %copy-start.3 = (f32[8]{0:T(128)S(1)}, f32[8]{0:T(128)}, u32[]{:S(2)}) copy-start(f32[8]{0:T(128)} %param.6) | copy-start | bytes 100
  11.4 0.7 %copy-start.4 = (s32[128]{0:T(128)S(1)}, s32[128]{0:T(128)}, u32[]{:S(2)}) copy-start(s32[128]{0:T(128)} %param.7) | copy-start | bytes 1540
  22.9 0.7 %copy-start = (f32[32,24,128]{2,1,0:T(8,128)}, f32[32,24,128]{2,1,0:T(8,128)S(1)}, u32[]{:S(2)}) copy-start(f32[32,24,128]{2,1,0:T(8,128)S(1)} %all-to-all-done.all_ref) | copy-start | bytes 1179652

commit v2 on v0

v2 whole, which is shorter than its diff:
```python
import functools
import math

import jax
import jax.numpy as jnp
from jax import lax
from jax.experimental import pallas as pl
from jax.experimental.pallas import tpu as pltpu
from jax.sharding import PartitionSpec as P


ROOT_FIVE = 2.23606797749979
LN_TWO = math.log(2.0)
AXES = ("blk", "grp")
TINY = 1e-30
PARAMS = pltpu.CompilerParams(vmem_limit_bytes=32 << 20)
VMEM = pl.BlockSpec(memory_space=pltpu.VMEM)
FAST = jnp.bfloat16


def split3(x):
    high = x.astype(FAST)
    rest = x - high.astype(jnp.float32)
    middle = rest.astype(FAST)
    low = (rest - middle.astype(jnp.float32)).astype(FAST)
    return high, middle, low


def split2(x):
    high = x.astype(FAST)
    return high, (x - high.astype(jnp.float32)).astype(FAST)


def augment(points, own):
    parts = split3(points)
    squares = jnp.sum(points * points, 0, keepdims=True)
    row = lax.broadcasted_iota(jnp.int32, points.shape, 0)
    a, b, c = (part.astype(jnp.float32) for part in split3(jnp.broadcast_to(squares, points.shape)))
    zero = jnp.zeros(points.shape, jnp.float32)
    one = jnp.ones(points.shape, jnp.float32)
    three = jnp.where(row == 0, a, jnp.where(row == 1, b, jnp.where(row == 2, c, zero))).astype(FAST)
    ones = jnp.where(row < 3, one, zero).astype(FAST)
    if own:
        high, middle, low = (part * FAST(-2.0) for part in parts)
        rows = [high, high, middle, high, low, middle, three, ones]
    else:
        high, middle, low = parts
        rows = [high, middle, high, low, high, middle, ones, three]
    return jnp.concatenate(rows, 0)


def matern(dist):
    dist = jnp.maximum(dist, TINY)
    radius = dist * lax.rsqrt(dist)
    return ((LN_TWO / 3.0) * dist + 1.0 / LN_TWO + radius) * jnp.exp2(-radius)


def dot(a, b, over_a, over_b):
    return lax.dot_general(a, b, (((over_a,), (over_b,)), ((), ())), preferred_element_type=jnp.float32)


def lanes(blocks):
    return blocks[0] if len(blocks) == 1 else jnp.concatenate(blocks, 1)


def scaled(points, scale):
    return points / jnp.tile(scale, (1, points.shape[1] // scale.shape[1])) * (ROOT_FIVE / LN_TWO)


def add_columns(dim, own, scale, stack_ref, total, kept, where):
    count, _, size = stack_ref.shape
    points = lanes([stack_ref[k, 0:dim, :] for k in range(count)])
    vectors = lanes([stack_ref[k, dim:, :] for k in range(count)])
    high, low = split2(matern(dot(augment(scaled(points, scale), False), own, 0, 0)))
    at = pl.ds(where * count * size, count * size)
    kept[0][at, :] = high
    kept[1][at, :] = low
    v_high, v_low = split2(vectors)
    total = total + dot(jnp.concatenate([v_high, v_low], 0), high, 1, 0)
    return total + dot(jnp.concatenate([v_high, jnp.zeros_like(v_low)], 0), low, 1, 0)


def columns_kernel(dim, count, opening, final, settings_ref, packed_ref, *refs):
    scale = settings_ref[0:dim, :]
    if opening:
        rows, refs = refs[0:opening], refs[opening:]
        own = augment(scaled(lanes([row[0:dim, :] for row in rows]), scale), True)
    else:
        own, before, refs = refs[0][...], refs[1][...], refs[2:]
    stacks, outs = refs[0:count], refs[count:]
    rhs = packed_ref.shape[0] - dim
    total = jnp.zeros((2 * rhs, own.shape[1]), jnp.float32) if opening else before
    for place, stack in enumerate(stacks):
        total = add_columns(dim, own, scale, stack, total, outs[-2:], place)
    if opening and not final:
        outs[0][...] = own
    if final:
        sums_ref = outs[0]
        blocks, _, size = sums_ref.shape
        for k in range(blocks):
            at = slice(k * size, (k + 1) * size)
            part = LN_TWO * (total[0:rhs, at] + total[rhs:, at])
            if k == 0:
                part = part + settings_ref[dim : dim + 1, :] * packed_ref[dim:, :]
            sums_ref[k] = part
    else:
        outs[-3][...] = total


def close_kernel(dim, plan, place_of, *refs):
    first_ref, parts_ref = refs[-2:]
    shares, parts = plan[0]
    rows, sums, kept = refs[0:shares], refs[shares : shares + parts], refs[shares + parts : -2]
    rhs, size = first_ref.shape
    targets = lanes([row[dim:, :] for row in rows])
    first = lanes([sum((sums[m][k ^ m] for m in range(1, parts)), sums[0][k]) for k in range(shares)])
    first_ref[...] = first[:, 0:size]
    gammas = jnp.sum(targets * targets, 1, keepdims=True)
    deltas = jnp.sum(first * targets, 1, keepdims=True)
    lane = lax.broadcasted_iota(jnp.int32, (8, size), 1)
    pairs = jnp.zeros((8, size), jnp.float32)
    for k in range(rhs // 8):
        pairs = jnp.where(lane == 2 * k, gammas[8 * k : 8 * k + 8], pairs)
        pairs = jnp.where(lane == 2 * k + 1, deltas[8 * k : 8 * k + 8], pairs)
    f_high, f_low = split2(LN_TWO * first)
    both = jnp.concatenate([f_high, f_low], 0)
    here = place_of()
    masks = iter(plan[1])
    for source in range(0, len(kept), 2):
        part = dot(both, kept[source][...], 1, 1)
        part = part[0:rhs, :] + part[rhs:, :] + dot(f_high, kept[source + 1][...], 1, 1)
        for k in range(part.shape[1] // size):
            to = here ^ next(masks)
            parts_ref[to, 0:rhs, :] = part[:, k * size : (k + 1) * size]
            parts_ref[to, rhs:, :] = pairs


def end_kernel(dim, settings_ref, packed_ref, first_ref, parts_ref, solution_ref, residual_ref, image_ref):
    rhs = first_ref.shape[0]
    total = sum((parts_ref[k] for k in range(1, parts_ref.shape[0])), parts_ref[0])
    first = first_ref[...]
    targets = packed_ref[dim:, :]
    further = total[0:rhs, :] + settings_ref[dim : dim + 1, :] * first
    gammas = jnp.concatenate([total[rhs:, 2 * k : 2 * k + 1] for k in range(rhs // 8)], 0)
    deltas = jnp.concatenate([total[rhs:, 2 * k + 1 : 2 * k + 2] for k in range(rhs // 8)], 0)
    alphas = gammas / deltas
    solution_ref[...] = alphas * targets
    residual_ref[...] = targets - alphas * first
    image_ref[...] = first - alphas * further


def call(body, operands, shapes, flops):
    return pl.pallas_call(
        body,
        in_specs=[VMEM] * len(operands),
        out_specs=tuple(VMEM for _ in shapes),
        out_shape=tuple(jax.ShapeDtypeStruct(shape, dtype) for shape, dtype in shapes),
        compiler_params=PARAMS,
        cost_estimate=pl.CostEstimate(flops=flops, transcendentals=0, bytes_accessed=0),
    )(*operands)


def layout(blk, grp):
    core = math.gcd(blk, 2)
    line = math.gcd(grp, 4)
    far = math.gcd(line, 2)
    rest = grp // line
    part = grp // far
    plane = [b * core * grp + r for b in range(blk // core) for r in range(rest)]
    return core, line // far, far, rest, part, plane


def on_device(blk, grp, design, lengthscales, counts, noise_base, targets):
    dim, size = design.shape
    rhs = targets.shape[0]
    devices = blk * grp
    core, near, far, rest, part, plane = layout(blk, grp)

    def swap(value, mask):
        return lax.ppermute(value, AXES, [(i, i ^ mask) for i in range(devices)])

    f32 = jnp.float32
    settings = jnp.concatenate([
        jnp.broadcast_to(lengthscales[:, None], (dim, size)),
        jnp.broadcast_to((noise_base[0] / counts.astype(f32))[None, :], (8, size)),
    ])
    packed = jnp.concatenate([design, targets])
    stack = [packed] + [swap(packed, k * rest) for k in range(1, near)]
    stack = jnp.stack(stack)
    stacks = [stack] + [swap(stack, mask) for mask in plane[1:]]
    rows = [packed]
    for steps, stride in ((far, part), (core, grp)):
        if steps == 2:
            rows += [swap(value, stride) for value in rows]
    shares = len(rows)
    points = shares * size
    third = -(-(len(stacks) - 1) // 3)
    groups = [stacks[0:1], stacks[1 : 1 + third], stacks[1 + third : 1 + 2 * third], stacks[1 + 2 * third :]]
    groups = [group for group in groups if group]
    kept = []
    own = total = None
    for number, group in enumerate(groups):
        final = number == len(groups) - 1
        shapes = [] if number or final else [((64, points), FAST)]
        shapes += [((shares, rhs, size), f32)] if final else [((2 * rhs, points), f32)]
        shapes += [((len(group) * near * size, points), FAST)] * 2
        found = call(
            functools.partial(columns_kernel, dim, len(group), 0 if number else shares, final),
            [settings, packed] + ([own, total] if number else rows) + group,
            shapes,
            200 * 80 * points * near * size * len(group),
        )
        *found, total, high, low = found
        own = found[0] if found else own
        kept += [high, low]
    turn = far
    if core == 2:
        total = total + jnp.roll(swap(total, grp), turn, 0)
    sums = [total] + ([swap(total, part)] if far == 2 else [])
    wide = near * rest
    columns = [mask // (core * grp) * wide + mask % grp + k * rest for mask in plane for k in range(near)]

    def place_of():
        return lax.axis_index("blk") // core * wide + lax.axis_index("grp") % wide

    members = blk // core * wide
    first, parts = call(
        functools.partial(close_kernel, dim, ((shares, len(sums)), columns), place_of),
        rows + sums + kept,
        [((rhs, size), f32), ((members, rhs + 8, size), f32)],
        200 * 80 * points * size,
    )
    teams = [
        [(b * core + c) * grp + f * part + r for b in range(blk // core) for r in range(part)]
        for c in range(core)
        for f in range(far)
    ]
    parts = lax.all_to_all(parts, AXES, 0, 0, axis_index_groups=teams)
    return call(functools.partial(end_kernel, dim), [settings, packed, first, parts], [((rhs, size), f32)] * 3, 1)


def solution(mesh):
    in_specs = (P(None, AXES), P(), P(AXES), P(), P(None, AXES))
    out_specs = (P(None, AXES), P(None, AXES), P(None, AXES))
    blk, grp = mesh.shape["blk"], mesh.shape["grp"]

    def body(*arguments):
        return on_device(blk, grp, *arguments)

    return jax.shard_map(body, mesh=mesh, in_specs=in_specs, out_specs=out_specs, check_vma=False)
```

time: 168 us -> 34.6 us (0.21)
  blocking collectives: 151 us -> 8.67 us
  matrix products: 12.4 us -> 0 us
  starting transfers between devices: 0 us -> 11.8 us
  waiting for transfers between devices: 0 us -> 6.64 us
  Pallas kernels: 0 us -> 3.72 us
    all_gather x6 -> x0, blocking collectives: 111 us -> none  [the longest x2 61.1 us: operator_apply(): lax.all_gather(direction, 'grp', axis=1, tiled=True)]
    psum x1 -> x0, blocking collectives: 39.5 us -> none  [on_device(): gammas, deltas = lax.psum((local_gammas, local_deltas), ('blk', 'grp'))]
    dot_general x8 -> x0, matrix products: 12.4 us -> none  [the longest x4 7.95 us: advance(): jnp.einsum('dr,dc->rc', own_scaled, chosen, precision=lax.Precision.HIGHEST)]
    ppermute x0 -> x9, starting transfers between devices: none -> 11.8 us  [swap(): return lax.ppermute(value, AXES, [(i, i ^ mask) for i in range(devices)])]
    all_to_all x0 -> x1, blocking collectives: none -> 8.67 us  [on_device(): parts = lax.all_to_all(parts, AXES, 0, 0, axis_index_groups=teams)]
    ppermute x0 -> x9, waiting for transfers between devices: none -> 6.64 us  [swap(): return lax.ppermute(value, AXES, [(i, i ^ mask) for i in range(devices)])]
    pallas_call x0 -> x6, Pallas kernels: none -> 3.72 us  [call(): pl.pallas_call(body, in_specs=[VMEM] * len(operands), out_specs=tuple((VM...]
  transfers between devices with their start and end apart: 0 -> 9, of which waited for: 0 -> 3; matrix products, arithmetic and copies ran while one was open for 0% -> 0% of each run, Pallas kernels for 0% -> 5%
where the time goes in v2:
time: 34.6 us; the launch traced here: 34.3 us
  starting transfers between devices  11.8 us (34%)
  blocking collectives  8.67 us (25%)
  waiting for transfers between devices  6.64 us (19%)
  Pallas kernels  3.72 us (11%)
  local copies, waits for them, and re-layouts  2.01 us (6%)
  between operations  1.34 us (4%)
    ppermute x9, starting transfers between devices, swap(): return lax.ppermute(value, AXES, [(i, i ^ mask) for i in range(devices)])  11.8 us
    all_to_all x1, blocking collectives, on_device(): parts = lax.all_to_all(parts, AXES, 0, 0, axis_index_groups=teams)  8.67 us
    ppermute x9, waiting for transfers between devices, swap(): return lax.ppermute(value, AXES, [(i, i ^ mask) for i in range(devices)])  6.64 us
    pallas_call x6, Pallas kernels, call(): pl.pallas_call(body, in_specs=[VMEM] * len(operands), out_specs=tuple((VM...  3.72 us
    unnamed x7, local copies, waits for them, and re-layouts  2 us
  transfers between devices with their start and end apart: 9, of which 3 were waited for; matrix products, arithmetic and copies ran while one was open for 0% of the time, Pallas kernels for 5%

profile of v2, /device:TPU:0, one launch (start us, length us, event | category | flops | bytes accessed | tf_op | source)
XLA Modules:
  0.0 34.3 jit_solution(16123498465482881257)
XLA Ops:
  0.6 0.0 copy-start
  0.6 0.7 %constant_dynamic-update-slice_fusion.1 = f32[24,128]{1,0:T(8,128)S(1)} fusion(f32[8,128]{1,0:T(8,128)} %param.5), kind=kLoop, calls=%fused_computation.4 | loop fusion | bytes 8192
  1.3 0.0 copy-done
  1.3 3.1 %collective-permute-start.3 = (f32[24,128]{1,0:T(8,128)S(1)}, f32[24,128]{1,0:T(8,128)S(1)}, u32[]{:S(2)}, u32[]{:S(2)}) collective-permute-start(f32[24,128]{1,0:T(8,128)S(1)} %constant_dynamic-update-slice_fusion.packed_ref.refs_0_), channel_id=1, source_target_pairs={{0,2},{1,3},{2,0},{3,1},{4,6},{5,7},{6,4},{7,5},{8,10},{9,11},{10,... | collective-permute-start | bytes 36872 | tf_op jit(solution)/shard_map/ppermute | solution.py:180
  4.4 0.0 collective-permute-start.1
  4.4 2.6 %collective-permute-start = (f32[24,128]{1,0:T(8,128)S(1)}, f32[24,128]{1,0:T(8,128)S(1)}, u32[]{:S(2)}, u32[]{:S(2)}) collective-permute-start(f32[24,128]{1,0:T(8,128)S(1)} %constant_dynamic-update-slice_fusion.packed_ref.refs_0_), channel_id=1, source_target_pairs={{0,4},{1,5},{2,6},{3,7},{4,0},{5,1},{6,2},{7,3},{8,12},{9,13},{10,... | collective-permute-start | bytes 36872 | tf_op jit(solution)/shard_map/ppermute | solution.py:180
  7.6 0.0 copy-start.1
  7.6 0.6 %copy-done.1 = s32[128]{0:T(128)S(1)} copy-done((s32[128]{0:T(128)S(1)}, s32[128]{0:T(128)}, u32[]{:S(2)}) %copy-start.1) | copy-done | bytes 536
  8.3 0.6 %copy-done.2 = f32[8]{0:T(128)S(1)} copy-done((f32[8]{0:T(128)S(1)}, f32[8]{0:T(128)}, u32[]{:S(2)}) %copy-start.2) | copy-done | bytes 56
  9.0 0.1 pad_maximum_fusion.1.settings_ref
  9.0 0.0 collective-permute-done.refs_1_
  9.0 0.2 collective-permute-start.2
  9.3 0.0 collective-permute-done.3
  9.3 2.4 %collective-permute-start.6 = (f32[2,24,128]{2,1,0:T(8,128)S(1)}, f32[2,24,128]{2,1,0:T(8,128)S(1)}, u32[]{:S(2)}, u32[]{:S(2)}) collective-permute-start(f32[2,24,128]{2,1,0:T(8,128)S(1)} %pad_maximum_fusion.refs_4_), channel_id=1, source_target_pairs={{0,17},{1,16},{2,19},{3,18},{4,21},{5,20},{6,23},{7,22},{8,25},{9,... | collective-permute-start | bytes 73736 | tf_op jit(solution)/shard_map/ppermute | solution.py:180
  11.7 0.5 %collective-permute-start.5 = (f32[2,24,128]{2,1,0:T(8,128)S(1)}, f32[2,24,128]{2,1,0:T(8,128)S(1)}, u32[]{:S(2)}, u32[]{:S(2)}) collective-permute-start(f32[2,24,128]{2,1,0:T(8,128)S(1)} %pad_maximum_fusion.refs_4_), channel_id=1, source_target_pairs={{0,16},{1,17},{2,18},{3,19},{4,20},{5,21},{6,22},{7,23},{8,24},{9,... | collective-permute-start | bytes 73736 | tf_op jit(solution)/shard_map/ppermute | solution.py:180
  12.3 0.5 %collective-permute-start.4 = (f32[2,24,128]{2,1,0:T(8,128)S(1)}, f32[2,24,128]{2,1,0:T(8,128)S(1)}, u32[]{:S(2)}, u32[]{:S(2)}) collective-permute-start(f32[2,24,128]{2,1,0:T(8,128)S(1)} %pad_maximum_fusion.refs_4_), channel_id=1, source_target_pairs={{0,1},{1,0},{2,3},{3,2},{4,5},{5,4},{6,7},{7,6},{8,9},{9,8},{10,11... | collective-permute-start | bytes 73736 | tf_op jit(solution)/shard_map/ppermute | solution.py:180
  12.8 0.0 collective-permute-done.1.refs_2_
  12.8 0.0 collective-permute-done.2.refs_3_
  12.8 0.6 %shard_map.76 = (bf16[64,512]{1,0:T(8,128)(2,1)S(1)}, f32[32,512]{1,0:T(8,128)S(1)}, bf16[256,512]{1,0:T(8,128)(2,1)S(1)}, bf16[256,512]{1,0:T(8,128)(2,1)S(1)}) custom-call(f32[16,128]{1,0:T(8,128)S(1)} %pad_maximum_fusion.1.settings_ref, f32[24,128]{1,0:T(8,128)S(1)} %constant_dynamic-update-slice_fusion.packed_ref.refs_0_, ...), custom_call_target="tpu_custom_call" | custom-call | flops 2097152000 | tf_op jit(solution)/shard_map/pallas_call | solution.py:153
  13.4 2.7 %collective-permute-done.4.refs_2_ = f32[2,24,128]{2,1,0:T(8,128)S(1)} collective-permute-done((f32[2,24,128]{2,1,0:T(8,128)S(1)}, f32[2,24,128]{2,1,0:T(8,128)S(1)}, u32[]{:S(2)}, u32[]{:S(2)}) %collective-permute-start.4) | collective-permute-done | bytes 24608 | tf_op jit(solution)/shard_map/ppermute | solution.py:180
  16.1 0.5 %shard_map.77 = (f32[32,512]{1,0:T(8,128)S(1)}, bf16[256,512]{1,0:T(8,128)(2,1)S(1)}, bf16[256,512]{1,0:T(8,128)(2,1)S(1)}) custom-call(f32[16,128]{1,0:T(8,128)S(1)} %pad_maximum_fusion.1.settings_ref, f32[24,128]{1,0:T(8,128)S(1)} %constant_dynamic-update-slice_fusion.packed_ref.refs_0_, bf16[64,512]{1,0:T(8,128)(2,1)S(1)} %get-tuple-element.18.refs_0_, ...), custom_call_target="tpu_custom_call" | custom-call | flops 2097152000 | tf_op jit(solution)/shard_map/pallas_call | solution.py:153
  16.6 0.0 collective-permute-done.5.refs_2_
  16.7 0.5 %shard_map.78 = (f32[32,512]{1,0:T(8,128)S(1)}, bf16[256,512]{1,0:T(8,128)(2,1)S(1)}, bf16[256,512]{1,0:T(8,128)(2,1)S(1)}) custom-call(f32[16,128]{1,0:T(8,128)S(1)} %pad_maximum_fusion.1.settings_ref, f32[24,128]{1,0:T(8,128)S(1)} %constant_dynamic-update-slice_fusion.packed_ref.refs_0_, bf16[64,512]{1,0:T(8,128)(2,1)S(1)} %get-tuple-element.18.refs_0_, ...), custom_call_target="tpu_custom_call" | custom-call | flops 2097152000 | tf_op jit(solution)/shard_map/pallas_call | solution.py:153
  17.2 0.0 collective-permute-done.6.refs_2_
  17.2 0.6 %shard_map.79 = (f32[4,16,128]{2,1,0:T(8,128)S(1)}, bf16[256,512]{1,0:T(8,128)(2,1)S(1)}, bf16[256,512]{1,0:T(8,128)(2,1)S(1)}) custom-call(f32[16,128]{1,0:T(8,128)S(1)} %pad_maximum_fusion.1.settings_ref, f32[24,128]{1,0:T(8,128)S(1)} %constant_dynamic-update-slice_fusion.packed_ref.refs_0_, bf16[64,512]{1,0:T(8,128)(2,1)S(1)} %get-tuple-element.18.refs_0_, ...), custom_call_target="tpu_custom_call" | custom-call | flops 2097152000 | tf_op jit(solution)/shard_map/pallas_call | solution.py:153
  17.8 0.0 collective-permute-start.7
  17.8 1.2 %collective-permute-done.7 = f32[4,16,128]{2,1,0:T(8,128)S(1)} collective-permute-done((f32[4,16,128]{2,1,0:T(8,128)S(1)}, f32[4,16,128]{2,1,0:T(8,128)S(1)}, u32[]{:S(2)}, u32[]{:S(2)}) %collective-permute-start.7) | collective-permute-done | bytes 32800 | tf_op jit(solution)/shard_map/ppermute | solution.py:180
  19.0 2.4 %collective-permute-start.8 = (f32[4,16,128]{2,1,0:T(8,128)S(1)}, f32[4,16,128]{2,1,0:T(8,128)S(1)}, u32[]{:S(2)}, u32[]{:S(2)}) collective-permute-start(f32[4,16,128]{2,1,0:T(8,128)S(1)} %maximum_add_fusion.refs_4_), channel_id=1, source_target_pairs={{0,4},{1,5},{2,6},{3,7},{4,0},{5,1},{6,2},{7,3},{8,12},{9,13},{10,... | collective-permute-start | bytes 98312 | tf_op jit(solution)/shard_map/ppermute | solution.py:180
  21.5 2.7 %collective-permute-done.8.refs_5_ = f32[4,16,128]{2,1,0:T(8,128)S(1)} collective-permute-done((f32[4,16,128]{2,1,0:T(8,128)S(1)}, f32[4,16,128]{2,1,0:T(8,128)S(1)}, u32[]{:S(2)}, u32[]{:S(2)}) %collective-permute-start.8) | collective-permute-done | bytes 32800 | tf_op jit(solution)/shard_map/ppermute | solution.py:180
  24.1 0.7 %shard_map.80 = (f32[16,128]{1,0:T(8,128)S(1)}, f32[8,24,128]{2,1,0:T(8,128)S(1)}) custom-call(f32[24,128]{1,0:T(8,128)S(1)} %constant_dynamic-update-slice_fusion.packed_ref.refs_0_, f32[24,128]{1,0:T(8,128)S(1)} %collective-permute-done.refs_1_, f32[24,128]{1,0:T(8,128)S(1)} %collective-permute-done.1.refs_2_, ...), custom_call_target="tpu_custom_call" | custom-call | flops 1048576000 | tf_op jit(solution)/shard_map/pallas_call | solution.py:153
  24.8 8.7 %all_to_all.5.parts_ref = f32[8,24,128]{2,1,0:T(8,128)S(1)} all-to-all(f32[8,24,128]{2,1,0:T(8,128)S(1)} %get-tuple-element.32), channel_id=1, replica_groups={{0,1,2,3,16,17,18,19},{4,5,6,7,20,21,22,23},{8,9,10,11,24,25,26,27},{12..., dimensions={0} | all-to-all | bytes 196608 | tf_op jit(solution)/shard_map/all_to_all | solution.py:238
  33.5 0.8 %shard_map.81 = (f32[16,128]{1,0:T(8,128)}, f32[16,128]{1,0:T(8,128)}, f32[16,128]{1,0:T(8,128)}) custom-call(f32[16,128]{1,0:T(8,128)S(1)} %pad_maximum_fusion.1.settings_ref, f32[24,128]{1,0:T(8,128)S(1)} %constant_dynamic-update-slice_fusion.packed_ref.refs_0_, f32[16,128]{1,0:T(8,128)S(1)} %get-tuple-element.31.first_ref, ...), custom_call_target="tpu_custom_call" | custom-call | flops 1 | tf_op jit(solution)/shard_map/pallas_call | solution.py:153
  (8 shorter events, 0.0 us)
Async XLA Ops:
  0.6 0.7 %copy-start = (f32[16,128]{1,0:T(8,128)S(1)}, f32[16,128]{1,0:T(8,128)}, u32[]{:S(2)}) copy-start(f32[16,128]{1,0:T(8,128)} %param.9) | copy-start | bytes 24580
  1.3 7.9 %collective-permute-start.3 = (f32[24,128]{1,0:T(8,128)S(1)}, f32[24,128]{1,0:T(8,128)S(1)}, u32[]{:S(2)}, u32[]{:S(2)}) collective-permute-start(f32[24,128]{1,0:T(8,128)S(1)} %constant_dynamic-update-slice_fusion.packed_ref.refs_0_), channel_id=1, source_target_pairs={{0,2},{1,3},{2,0},{3,1},{4,6},{5,7},{6,4},{7,5},{8,10},{9,11},{10,... | collective-permute-start | bytes 36872 | tf_op jit(solution)/shard_map/ppermute | solution.py:180
  4.4 8.4 %collective-permute-start.1 = (f32[24,128]{1,0:T(8,128)S(1)}, f32[24,128]{1,0:T(8,128)S(1)}, u32[]{:S(2)}, u32[]{:S(2)}) collective-permute-start(f32[24,128]{1,0:T(8,128)S(1)} %constant_dynamic-update-slice_fusion.packed_ref.refs_0_), channel_id=1, source_target_pairs={{0,8},{1,9},{2,10},{3,11},{4,12},{5,13},{6,14},{7,15},{8,0},{9,1},... | collective-permute-start | bytes 36872 | tf_op jit(solution)/shard_map/ppermute | solution.py:180
  4.4 4.6 %collective-permute-start = (f32[24,128]{1,0:T(8,128)S(1)}, f32[24,128]{1,0:T(8,128)S(1)}, u32[]{:S(2)}, u32[]{:S(2)}) collective-permute-start(f32[24,128]{1,0:T(8,128)S(1)} %constant_dynamic-update-slice_fusion.packed_ref.refs_0_), channel_id=1, source_target_pairs={{0,4},{1,5},{2,6},{3,7},{4,0},{5,1},{6,2},{7,3},{8,12},{9,13},{10,... | collective-permute-start | bytes 36872 | tf_op jit(solution)/shard_map/ppermute | solution.py:180
  7.6 0.7 %copy-start.1 = (s32[128]{0:T(128)S(1)}, s32[128]{0:T(128)}, u32[]{:S(2)}) copy-start(s32[128]{0:T(128)} %param.7) | copy-start | bytes 1540
  8.3 0.7 %copy-start.2 = (f32[8]{0:T(128)S(1)}, f32[8]{0:T(128)}, u32[]{:S(2)}) copy-start(f32[8]{0:T(128)} %param.6) | copy-start | bytes 100
  9.0 3.7 %collective-permute-start.2 = (f32[24,128]{1,0:T(8,128)S(1)}, f32[24,128]{1,0:T(8,128)S(1)}, u32[]{:S(2)}, u32[]{:S(2)}) collective-permute-start(f32[24,128]{1,0:T(8,128)S(1)} %collective-permute-done.refs_1_), channel_id=1, source_target_pairs={{0,8},{1,9},{2,10},{3,11},{4,12},{5,13},{6,14},{7,15},{8,0},{9,1},... | collective-permute-start | bytes 36872 | tf_op jit(solution)/shard_map/ppermute | solution.py:180
  9.3 7.9 %collective-permute-start.6 = (f32[2,24,128]{2,1,0:T(8,128)S(1)}, f32[2,24,128]{2,1,0:T(8,128)S(1)}, u32[]{:S(2)}, u32[]{:S(2)}) collective-permute-start(f32[2,24,128]{2,1,0:T(8,128)S(1)} %pad_maximum_fusion.refs_4_), channel_id=1, source_target_pairs={{0,17},{1,16},{2,19},{3,18},{4,21},{5,20},{6,23},{7,22},{8,25},{9,... | collective-permute-start | bytes 73736 | tf_op jit(solution)/shard_map/ppermute | solution.py:180
  11.7 4.9 %collective-permute-start.5 = (f32[2,24,128]{2,1,0:T(8,128)S(1)}, f32[2,24,128]{2,1,0:T(8,128)S(1)}, u32[]{:S(2)}, u32[]{:S(2)}) collective-permute-start(f32[2,24,128]{2,1,0:T(8,128)S(1)} %pad_maximum_fusion.refs_4_), channel_id=1, source_target_pairs={{0,16},{1,17},{2,18},{3,19},{4,20},{5,21},{6,22},{7,23},{8,24},{9,... | collective-permute-start | bytes 73736 | tf_op jit(solution)/shard_map/ppermute | solution.py:180
  12.3 3.8 %collective-permute-start.4 = (f32[2,24,128]{2,1,0:T(8,128)S(1)}, f32[2,24,128]{2,1,0:T(8,128)S(1)}, u32[]{:S(2)}, u32[]{:S(2)}) collective-permute-start(f32[2,24,128]{2,1,0:T(8,128)S(1)} %pad_maximum_fusion.refs_4_), channel_id=1, source_target_pairs={{0,1},{1,0},{2,3},{3,2},{4,5},{5,4},{6,7},{7,6},{8,9},{9,8},{10,11... | collective-permute-start | bytes 73736 | tf_op jit(solution)/shard_map/ppermute | solution.py:180
  17.8 1.2 %collective-permute-start.7 = (f32[4,16,128]{2,1,0:T(8,128)S(1)}, f32[4,16,128]{2,1,0:T(8,128)S(1)}, u32[]{:S(2)}, u32[]{:S(2)}) collective-permute-start(f32[4,16,128]{2,1,0:T(8,128)S(1)} %get-tuple-element.22), channel_id=1, source_target_pairs={{0,8},{1,9},{2,10},{3,11},{4,12},{5,13},{6,14},{7,15},{8,0},{9,1},... | collective-permute-start | bytes 98312 | tf_op jit(solution)/shard_map/ppermute | solution.py:180
  19.0 5.1 %collective-permute-start.8 = (f32[4,16,128]{2,1,0:T(8,128)S(1)}, f32[4,16,128]{2,1,0:T(8,128)S(1)}, u32[]{:S(2)}, u32[]{:S(2)}) collective-permute-start(f32[4,16,128]{2,1,0:T(8,128)S(1)} %maximum_add_fusion.refs_4_), channel_id=1, source_target_pairs={{0,4},{1,5},{2,6},{3,7},{4,0},{5,1},{6,2},{7,3},{8,12},{9,13},{10,... | collective-permute-start | bytes 98312 | tf_op jit(solution)/shard_map/ppermute | solution.py:180

commit v3 on v2

--- a/solution.py
+++ b/solution.py
@@ -67,12 +67,12 @@
     return points / jnp.tile(scale, (1, points.shape[1] // scale.shape[1])) * (ROOT_FIVE / LN_TWO)
 
 
-def add_columns(dim, own, scale, stack_ref, total, kept, where):
-    count, _, size = stack_ref.shape
-    points = lanes([stack_ref[k, 0:dim, :] for k in range(count)])
-    vectors = lanes([stack_ref[k, dim:, :] for k in range(count)])
+def add_columns(dim, own, scale, stacks, total, kept, start):
+    count, _, size = stacks[0].shape
+    points = lanes([stack[k, 0:dim, :] for stack in stacks for k in range(count)])
+    vectors = lanes([stack[k, dim:, :] for stack in stacks for k in range(count)])
     high, low = split2(matern(dot(augment(scaled(points, scale), False), own, 0, 0)))
-    at = pl.ds(where * count * size, count * size)
+    at = pl.ds(start * count * size, len(stacks) * count * size)
     kept[0][at, :] = high
     kept[1][at, :] = low
     v_high, v_low = split2(vectors)
@@ -80,18 +80,20 @@
     return total + dot(jnp.concatenate([v_high, jnp.zeros_like(v_low)], 0), low, 1, 0)
 
 
-def columns_kernel(dim, count, opening, final, settings_ref, packed_ref, *refs):
+def columns_kernel(dim, count, opening, final, settings_ref, *refs):
     scale = settings_ref[0:dim, :]
+    if final:
+        packed_ref, noise_ref, refs = refs[0], refs[1], refs[2:]
     if opening:
         rows, refs = refs[0:opening], refs[opening:]
         own = augment(scaled(lanes([row[0:dim, :] for row in rows]), scale), True)
     else:
         own, before, refs = refs[0][...], refs[1][...], refs[2:]
     stacks, outs = refs[0:count], refs[count:]
-    rhs = packed_ref.shape[0] - dim
+    rhs = stacks[0].shape[1] - dim
     total = jnp.zeros((2 * rhs, own.shape[1]), jnp.float32) if opening else before
-    for place, stack in enumerate(stacks):
-        total = add_columns(dim, own, scale, stack, total, outs[-2:], place)
+    for start in range(0, count, 2):
+        total = add_columns(dim, own, scale, stacks[start : start + 2], total, outs[-2:], start)
     if opening and not final:
         outs[0][...] = own
     if final:
@@ -101,7 +103,7 @@
             at = slice(k * size, (k + 1) * size)
             part = LN_TWO * (total[0:rhs, at] + total[rhs:, at])
             if k == 0:
-                part = part + settings_ref[dim : dim + 1, :] * packed_ref[dim:, :]
+                part = part + noise_ref[0:1, :] * packed_ref[dim:, :]
             sums_ref[k] = part
     else:
         outs[-3][...] = total
@@ -135,12 +137,12 @@
             parts_ref[to, rhs:, :] = pairs
 
 
-def end_kernel(dim, settings_ref, packed_ref, first_ref, parts_ref, solution_ref, residual_ref, image_ref):
+def end_kernel(dim, noise_ref, packed_ref, first_ref, parts_ref, solution_ref, residual_ref, image_ref):
     rhs = first_ref.shape[0]
     total = sum((parts_ref[k] for k in range(1, parts_ref.shape[0])), parts_ref[0])
     first = first_ref[...]
     targets = packed_ref[dim:, :]
-    further = total[0:rhs, :] + settings_ref[dim : dim + 1, :] * first
+    further = total[0:rhs, :] + noise_ref[0:1, :] * first
     gammas = jnp.concatenate([total[rhs:, 2 * k : 2 * k + 1] for k in range(rhs // 8)], 0)
     deltas = jnp.concatenate([total[rhs:, 2 * k + 1 : 2 * k + 2] for k in range(rhs // 8)], 0)
     alphas = gammas / deltas
@@ -180,10 +182,8 @@
         return lax.ppermute(value, AXES, [(i, i ^ mask) for i in range(devices)])
 
     f32 = jnp.float32
-    settings = jnp.concatenate([
-        jnp.broadcast_to(lengthscales[:, None], (dim, size)),
-        jnp.broadcast_to((noise_base[0] / counts.astype(f32))[None, :], (8, size)),
-    ])
+    settings = jnp.broadcast_to(lengthscales[:, None], (dim, size))
+    noise = jnp.broadcast_to((noise_base[0] / counts.astype(f32))[None, :], (8, size))
     packed = jnp.concatenate([design, targets])
     stack = [packed] + [swap(packed, k * rest) for k in range(1, near)]
     stack = jnp.stack(stack)
@@ -194,8 +194,9 @@
             rows += [swap(value, stride) for value in rows]
     shares = len(rows)
     points = shares * size
-    third = -(-(len(stacks) - 1) // 3)
-    groups = [stacks[0:1], stacks[1 : 1 + third], stacks[1 + third : 1 + 2 * third], stacks[1 + 2 * third :]]
+    half = -(-len(stacks) // 2)
+    third = -(-3 * len(stacks) // 4)
+    groups = [stacks[0:half], stacks[half:third], stacks[third:]]
     groups = [group for group in groups if group]
     kept = []
     own = total = None
@@ -206,7 +207,7 @@
         shapes += [((len(group) * near * size, points), FAST)] * 2
         found = call(
             functools.partial(columns_kernel, dim, len(group), 0 if number else shares, final),
-            [settings, packed] + ([own, total] if number else rows) + group,
+            [settings] + ([packed, noise] if final else []) + ([own, total] if number else rows) + group,
             shapes,
             200 * 80 * points * near * size * len(group),
         )
@@ -236,7 +237,7 @@
         for f in range(far)
     ]
     parts = lax.all_to_all(parts, AXES, 0, 0, axis_index_groups=teams)
-    return call(functools.partial(end_kernel, dim), [settings, packed, first, parts], [((rhs, size), f32)] * 3, 1)
+    return call(functools.partial(end_kernel, dim), [noise, packed, first, parts], [((rhs, size), f32)] * 3, 1)
 
 
 def solution(mesh):

time: 34.6 us -> 33.1 us (0.957)
  local copies, waits for them, and re-layouts: 2.01 us -> 0.79 us
  starting transfers between devices: 11.8 us -> 12.7 us
  waiting for transfers between devices: 6.64 us -> 6.01 us
    unnamed x7, local copies, waits for them, and re-layouts: 2 us -> 0.71 us
    ppermute x9, starting transfers between devices: 11.8 us -> 12.7 us  [swap(): return lax.ppermute(value, AXES, [(i, i ^ mask) for i in range(devices)])]
    ppermute x9, waiting for transfers between devices: 6.64 us -> 6.01 us  [swap(): return lax.ppermute(value, AXES, [(i, i ^ mask) for i in range(devices)])]
    pallas_call x6 -> x5, Pallas kernels: 3.72 us -> 3.47 us  [call(): pl.pallas_call(body, in_specs=[VMEM] * len(operands), out_specs=tuple((VM...]
  transfers between devices with their start and end apart: 9 -> 9, of which waited for: 3 -> 3; matrix products, arithmetic and copies ran while one was open for 0% -> 0% of each run, Pallas kernels for 5% -> 4%
where the time goes in v3:
time: 33.1 us; the launch traced here: 32.8 us
  starting transfers between devices  12.7 us (38%)
  blocking collectives  8.49 us (26%)
  waiting for transfers between devices  6.01 us (18%)
  Pallas kernels  3.47 us (10%)
  between operations  1.38 us (4%)
  local copies, waits for them, and re-layouts  0.79 us (2%)
    ppermute x9, starting transfers between devices, swap(): return lax.ppermute(value, AXES, [(i, i ^ mask) for i in range(devices)])  12.7 us
    all_to_all x1, blocking collectives, on_device(): parts = lax.all_to_all(parts, AXES, 0, 0, axis_index_groups=teams)  8.49 us
    ppermute x9, waiting for transfers between devices, swap(): return lax.ppermute(value, AXES, [(i, i ^ mask) for i in range(devices)])  6.01 us
    pallas_call x5, Pallas kernels, call(): pl.pallas_call(body, in_specs=[VMEM] * len(operands), out_specs=tuple((VM...  3.47 us
    unnamed x7, local copies, waits for them, and re-layouts  0.71 us
  transfers between devices with their start and end apart: 9, of which 3 were waited for; matrix products, arithmetic and copies ran while one was open for 0% of the time, Pallas kernels for 4%

profile of v3, /device:TPU:0, one launch (start us, length us, event | category | flops | bytes accessed | tf_op | source)
XLA Modules:
  0.0 32.8 jit_solution(8028031590932460880)
XLA Ops:
  0.6 0.0 copy-start
  0.6 0.7 %constant_dynamic-update-slice_fusion.1 = f32[24,128]{1,0:T(8,128)S(1)} fusion(f32[8,128]{1,0:T(8,128)} %param.5), kind=kLoop, calls=%fused_computation.3 | loop fusion | bytes 8192
  1.3 0.0 copy-done
  1.3 3.1 %collective-permute-start.3 = (f32[24,128]{1,0:T(8,128)S(1)}, f32[24,128]{1,0:T(8,128)S(1)}, u32[]{:S(2)}, u32[]{:S(2)}) collective-permute-start(f32[24,128]{1,0:T(8,128)S(1)} %constant_dynamic-update-slice_fusion.refs_0_.packed_ref), channel_id=1, source_target_pairs={{0,2},{1,3},{2,0},{3,1},{4,6},{5,7},{6,4},{7,5},{8,10},{9,11},{10,... | collective-permute-start | bytes 36872 | tf_op jit(solution)/shard_map/ppermute | solution.py:182
  4.4 0.0 collective-permute-start.1
  4.4 2.6 %collective-permute-start = (f32[24,128]{1,0:T(8,128)S(1)}, f32[24,128]{1,0:T(8,128)S(1)}, u32[]{:S(2)}, u32[]{:S(2)}) collective-permute-start(f32[24,128]{1,0:T(8,128)S(1)} %constant_dynamic-update-slice_fusion.refs_0_.packed_ref), channel_id=1, source_target_pairs={{0,4},{1,5},{2,6},{3,7},{4,0},{5,1},{6,2},{7,3},{8,12},{9,13},{10,... | collective-permute-start | bytes 36872 | tf_op jit(solution)/shard_map/ppermute | solution.py:182
  7.6 0.0 collective-permute-done.3
  7.7 0.0 copy-start.2
  7.7 1.6 %collective-permute-start.4 = (f32[2,24,128]{2,1,0:T(8,128)S(1)}, f32[2,24,128]{2,1,0:T(8,128)S(1)}, u32[]{:S(2)}, u32[]{:S(2)}) collective-permute-start(f32[2,24,128]{2,1,0:T(8,128)S(1)} %pad_maximum_fusion.refs_4_), channel_id=1, source_target_pairs={{0,1},{1,0},{2,3},{3,2},{4,5},{5,4},{6,7},{7,6},{8,9},{9,8},{10,11... | collective-permute-start | bytes 73736 | tf_op jit(solution)/shard_map/ppermute | solution.py:182
  9.3 0.0 collective-permute-done.refs_1_
  9.3 0.0 collective-permute-start.2
  9.3 0.0 copy-done.2
  9.3 0.0 copy-start.1
  9.3 2.2 %collective-permute-start.6 = (f32[2,24,128]{2,1,0:T(8,128)S(1)}, f32[2,24,128]{2,1,0:T(8,128)S(1)}, u32[]{:S(2)}, u32[]{:S(2)}) collective-permute-start(f32[2,24,128]{2,1,0:T(8,128)S(1)} %pad_maximum_fusion.refs_4_), channel_id=1, source_target_pairs={{0,17},{1,16},{2,19},{3,18},{4,21},{5,20},{6,23},{7,22},{8,25},{9,... | collective-permute-start | bytes 73736 | tf_op jit(solution)/shard_map/ppermute | solution.py:182
  11.5 0.5 %collective-permute-start.5 = (f32[2,24,128]{2,1,0:T(8,128)S(1)}, f32[2,24,128]{2,1,0:T(8,128)S(1)}, u32[]{:S(2)}, u32[]{:S(2)}) collective-permute-start(f32[2,24,128]{2,1,0:T(8,128)S(1)} %pad_maximum_fusion.refs_4_), channel_id=1, source_target_pairs={{0,16},{1,17},{2,18},{3,19},{4,20},{5,21},{6,22},{7,23},{8,24},{9,... | collective-permute-start | bytes 73736 | tf_op jit(solution)/shard_map/ppermute | solution.py:182
  12.1 0.0 collective-permute-done.1.refs_2_
  12.1 0.0 collective-permute-done.2.refs_3_
  12.1 0.0 collective-permute-done.4.refs_5_
  12.1 0.0 copy-done.1
  12.1 0.1 broadcast_in_dim.5.settings_ref
  12.2 0.9 %shard_map.76 = (bf16[64,512]{1,0:T(8,128)(2,1)S(1)}, f32[32,512]{1,0:T(8,128)S(1)}, bf16[512,512]{1,0:T(8,128)(2,1)S(1)}, bf16[512,512]{1,0:T(8,128)(2,1)S(1)}) custom-call(f32[8,128]{1,0:T(8,128)S(1)} %broadcast_in_dim.5.settings_ref, f32[24,128]{1,0:T(8,128)S(1)} %constant_dynamic-update-slice_fusion.refs_0_.packed_ref, ...), custom_call_target="tpu_custom_call" | custom-call | flops 4194304000 | tf_op jit(solution)/shard_map/pallas_call | solution.py:155
  13.1 2.3 %collective-permute-done.5.refs_2_ = f32[2,24,128]{2,1,0:T(8,128)S(1)} collective-permute-done((f32[2,24,128]{2,1,0:T(8,128)S(1)}, f32[2,24,128]{2,1,0:T(8,128)S(1)}, u32[]{:S(2)}, u32[]{:S(2)}) %collective-permute-start.5) | collective-permute-done | bytes 24608 | tf_op jit(solution)/shard_map/ppermute | solution.py:182
  15.4 0.6 %shard_map.77 = (f32[32,512]{1,0:T(8,128)S(1)}, bf16[256,512]{1,0:T(8,128)(2,1)S(1)}, bf16[256,512]{1,0:T(8,128)(2,1)S(1)}) custom-call(f32[8,128]{1,0:T(8,128)S(1)} %broadcast_in_dim.5.settings_ref, bf16[64,512]{1,0:T(8,128)(2,1)S(1)} %get-tuple-element.15.refs_0_.refs_2_, f32[32,512]{1,0:T(8,128)S(1)} %get-tuple-element.16.refs_1_, ...), custom_call_target="tpu_custom_call" | custom-call | flops 2097152000 | tf_op jit(solution)/shard_map/pallas_call | solution.py:155
  15.9 0.0 collective-permute-done.6.refs_4_
  15.9 0.6 %shard_map.78 = (f32[4,16,128]{2,1,0:T(8,128)S(1)}, bf16[256,512]{1,0:T(8,128)(2,1)S(1)}, bf16[256,512]{1,0:T(8,128)(2,1)S(1)}) custom-call(f32[8,128]{1,0:T(8,128)S(1)} %broadcast_in_dim.5.settings_ref, f32[24,128]{1,0:T(8,128)S(1)} %constant_dynamic-update-slice_fusion.refs_0_.packed_ref, f32[8,128]{1,0:T(8,128)S(1)} %broadcast_in_dim.4.refs_1_.noise_ref, ...), custom_call_target="tpu_custom_call" | custom-call | flops 2097152000 | tf_op jit(solution)/shard_map/pallas_call | solution.py:155
  16.5 0.0 collective-permute-start.7
  16.5 1.2 %collective-permute-done.7 = f32[4,16,128]{2,1,0:T(8,128)S(1)} collective-permute-done((f32[4,16,128]{2,1,0:T(8,128)S(1)}, f32[4,16,128]{2,1,0:T(8,128)S(1)}, u32[]{:S(2)}, u32[]{:S(2)}) %collective-permute-start.7) | collective-permute-done | bytes 32800 | tf_op jit(solution)/shard_map/ppermute | solution.py:182
  17.7 2.6 %collective-permute-start.8 = (f32[4,16,128]{2,1,0:T(8,128)S(1)}, f32[4,16,128]{2,1,0:T(8,128)S(1)}, u32[]{:S(2)}, u32[]{:S(2)}) collective-permute-start(f32[4,16,128]{2,1,0:T(8,128)S(1)} %maximum_add_fusion.refs_4_), channel_id=1, source_target_pairs={{0,4},{1,5},{2,6},{3,7},{4,0},{5,1},{6,2},{7,3},{8,12},{9,13},{10,... | collective-permute-start | bytes 98312 | tf_op jit(solution)/shard_map/ppermute | solution.py:182
  20.4 2.5 %collective-permute-done.8.refs_5_ = f32[4,16,128]{2,1,0:T(8,128)S(1)} collective-permute-done((f32[4,16,128]{2,1,0:T(8,128)S(1)}, f32[4,16,128]{2,1,0:T(8,128)S(1)}, u32[]{:S(2)}, u32[]{:S(2)}) %collective-permute-start.8) | collective-permute-done | bytes 32800 | tf_op jit(solution)/shard_map/ppermute | solution.py:182
  22.8 0.7 %shard_map.79 = (f32[16,128]{1,0:T(8,128)S(1)}, f32[8,24,128]{2,1,0:T(8,128)S(1)}) custom-call(f32[24,128]{1,0:T(8,128)S(1)} %constant_dynamic-update-slice_fusion.refs_0_.packed_ref, f32[24,128]{1,0:T(8,128)S(1)} %collective-permute-done.refs_1_, f32[24,128]{1,0:T(8,128)S(1)} %collective-permute-done.1.refs_2_, ...), custom_call_target="tpu_custom_call" | custom-call | flops 1048576000 | tf_op jit(solution)/shard_map/pallas_call | solution.py:155
  23.5 8.5 %all_to_all.5.parts_ref = f32[8,24,128]{2,1,0:T(8,128)S(1)} all-to-all(f32[8,24,128]{2,1,0:T(8,128)S(1)} %get-tuple-element.26), channel_id=1, replica_groups={{0,1,2,3,16,17,18,19},{4,5,6,7,20,21,22,23},{8,9,10,11,24,25,26,27},{12..., dimensions={0} | all-to-all | bytes 196608 | tf_op jit(solution)/shard_map/all_to_all | solution.py:239
  32.0 0.8 %shard_map.80 = (f32[16,128]{1,0:T(8,128)}, f32[16,128]{1,0:T(8,128)}, f32[16,128]{1,0:T(8,128)}) custom-call(f32[8,128]{1,0:T(8,128)S(1)} %broadcast_in_dim.4.refs_1_.noise_ref, f32[24,128]{1,0:T(8,128)S(1)} %constant_dynamic-update-slice_fusion.refs_0_.packed_ref, f32[16,128]{1,0:T(8,128)S(1)} %get-tuple-element.25.first_ref, ...), custom_call_target="tpu_custom_call" | custom-call | flops 1 | tf_op jit(solution)/shard_map/pallas_call | solution.py:155
  (6 shorter events, 0.0 us)
Async XLA Ops:
  0.6 0.7 %copy-start = (f32[16,128]{1,0:T(8,128)S(1)}, f32[16,128]{1,0:T(8,128)}, u32[]{:S(2)}) copy-start(f32[16,128]{1,0:T(8,128)} %param.9) | copy-start | bytes 24580
  1.3 6.3 %collective-permute-start.3 = (f32[24,128]{1,0:T(8,128)S(1)}, f32[24,128]{1,0:T(8,128)S(1)}, u32[]{:S(2)}, u32[]{:S(2)}) collective-permute-start(f32[24,128]{1,0:T(8,128)S(1)} %constant_dynamic-update-slice_fusion.refs_0_.packed_ref), channel_id=1, source_target_pairs={{0,2},{1,3},{2,0},{3,1},{4,6},{5,7},{6,4},{7,5},{8,10},{9,11},{10,... | collective-permute-start | bytes 36872 | tf_op jit(solution)/shard_map/ppermute | solution.py:182
  4.4 7.7 %collective-permute-start.1 = (f32[24,128]{1,0:T(8,128)S(1)}, f32[24,128]{1,0:T(8,128)S(1)}, u32[]{:S(2)}, u32[]{:S(2)}) collective-permute-start(f32[24,128]{1,0:T(8,128)S(1)} %constant_dynamic-update-slice_fusion.refs_0_.packed_ref), channel_id=1, source_target_pairs={{0,8},{1,9},{2,10},{3,11},{4,12},{5,13},{6,14},{7,15},{8,0},{9,1},... | collective-permute-start | bytes 36872 | tf_op jit(solution)/shard_map/ppermute | solution.py:182
  4.4 4.9 %collective-permute-start = (f32[24,128]{1,0:T(8,128)S(1)}, f32[24,128]{1,0:T(8,128)S(1)}, u32[]{:S(2)}, u32[]{:S(2)}) collective-permute-start(f32[24,128]{1,0:T(8,128)S(1)} %constant_dynamic-update-slice_fusion.refs_0_.packed_ref), channel_id=1, source_target_pairs={{0,4},{1,5},{2,6},{3,7},{4,0},{5,1},{6,2},{7,3},{8,12},{9,13},{10,... | collective-permute-start | bytes 36872 | tf_op jit(solution)/shard_map/ppermute | solution.py:182
  7.7 1.6 %copy-start.2 = (s32[128]{0:T(128)S(1)}, s32[128]{0:T(128)}, u32[]{:S(2)}) copy-start(s32[128]{0:T(128)} %param.7) | copy-start | bytes 1540
  7.7 4.4 %collective-permute-start.4 = (f32[2,24,128]{2,1,0:T(8,128)S(1)}, f32[2,24,128]{2,1,0:T(8,128)S(1)}, u32[]{:S(2)}, u32[]{:S(2)}) collective-permute-start(f32[2,24,128]{2,1,0:T(8,128)S(1)} %pad_maximum_fusion.refs_4_), channel_id=1, source_target_pairs={{0,1},{1,0},{2,3},{3,2},{4,5},{5,4},{6,7},{7,6},{8,9},{9,8},{10,11... | collective-permute-start | bytes 73736 | tf_op jit(solution)/shard_map/ppermute | solution.py:182
  9.3 2.8 %collective-permute-start.2 = (f32[24,128]{1,0:T(8,128)S(1)}, f32[24,128]{1,0:T(8,128)S(1)}, u32[]{:S(2)}, u32[]{:S(2)}) collective-permute-start(f32[24,128]{1,0:T(8,128)S(1)} %collective-permute-done.refs_1_), channel_id=1, source_target_pairs={{0,8},{1,9},{2,10},{3,11},{4,12},{5,13},{6,14},{7,15},{8,0},{9,1},... | collective-permute-start | bytes 36872 | tf_op jit(solution)/shard_map/ppermute | solution.py:182
  9.3 2.8 %copy-start.1 = (f32[8]{0:T(128)S(1)}, f32[8]{0:T(128)}, u32[]{:S(2)}) copy-start(f32[8]{0:T(128)} %param.6) | copy-start | bytes 100
  9.3 6.6 %collective-permute-start.6 = (f32[2,24,128]{2,1,0:T(8,128)S(1)}, f32[2,24,128]{2,1,0:T(8,128)S(1)}, u32[]{:S(2)}, u32[]{:S(2)}) collective-permute-start(f32[2,24,128]{2,1,0:T(8,128)S(1)} %pad_maximum_fusion.refs_4_), channel_id=1, source_target_pairs={{0,17},{1,16},{2,19},{3,18},{4,21},{5,20},{6,23},{7,22},{8,25},{9,... | collective-permute-start | bytes 73736 | tf_op jit(solution)/shard_map/ppermute | solution.py:182
  11.5 3.8 %collective-permute-start.5 = (f32[2,24,128]{2,1,0:T(8,128)S(1)}, f32[2,24,128]{2,1,0:T(8,128)S(1)}, u32[]{:S(2)}, u32[]{:S(2)}) collective-permute-start(f32[2,24,128]{2,1,0:T(8,128)S(1)} %pad_maximum_fusion.refs_4_), channel_id=1, source_target_pairs={{0,16},{1,17},{2,18},{3,19},{4,20},{5,21},{6,22},{7,23},{8,24},{9,... | collective-permute-start | bytes 73736 | tf_op jit(solution)/shard_map/ppermute | solution.py:182
  16.5 1.2 %collective-permute-start.7 = (f32[4,16,128]{2,1,0:T(8,128)S(1)}, f32[4,16,128]{2,1,0:T(8,128)S(1)}, u32[]{:S(2)}, u32[]{:S(2)}) collective-permute-start(f32[4,16,128]{2,1,0:T(8,128)S(1)} %get-tuple-element.18), channel_id=1, source_target_pairs={{0,8},{1,9},{2,10},{3,11},{4,12},{5,13},{6,14},{7,15},{8,0},{9,1},... | collective-permute-start | bytes 98312 | tf_op jit(solution)/shard_map/ppermute | solution.py:182
  17.7 5.1 %collective-permute-start.8 = (f32[4,16,128]{2,1,0:T(8,128)S(1)}, f32[4,16,128]{2,1,0:T(8,128)S(1)}, u32[]{:S(2)}, u32[]{:S(2)}) collective-permute-start(f32[4,16,128]{2,1,0:T(8,128)S(1)} %maximum_add_fusion.refs_4_), channel_id=1, source_target_pairs={{0,4},{1,5},{2,6},{3,7},{4,0},{5,1},{6,2},{7,3},{8,12},{9,13},{10,... | collective-permute-start | bytes 98312 | tf_op jit(solution)/shard_map/ppermute | solution.py:182
